TPU v7x, 32 devices: a whole 2x2x4 slice. The times are simulated.
32 devices in a mesh: cp: 4 (over z), tp: 8 (over y, x, core).
Axes of the slice: x: 2, y: 2, z: 4, core: 2. Of those that a mesh axis runs over, the one named last changes fastest.
Arguments:
- checkpoint: bfloat16 [2048, 8192], P('cp', 'tp'), may hold values from -6 to 6
- norm_gain: float32 [8192], replicated, may hold values from 0.1 to 1.9
- query_weight: bfloat16 [8192, 8192], P(None, 'tp'), may hold values from -4 to 4
- key_weight: bfloat16 [8192, 1024], P(None, 'tp'), may hold values from -1 to 1
- value_weight: bfloat16 [8192, 1024], P(None, 'tp'), may hold values from -0.0625 to 0.0625
- output_weight: bfloat16 [8192, 8192], P('tp'), may hold values from -0.09375 to 0.09375
- block_order: int32 [8], replicated, may hold values from 0 to 7, each once
Outputs:
- projected: bfloat16 [2048, 8192], P('cp', 'tp')
- log_normalizer: float32 [64, 2048], P('tp', 'cp')
Inputs may be any that keep to these rules, and one draw needn't show every extreme that they name: `block_order`: each of 0 to 7 once.
All inputs are finite; a program needn't handle non-finite values.
Results may differ from a plain program's by a relative error of at most 0.019.
Values may be sent and summed in bfloat16 or wider, within the bound.
A program may use at most 128 MiB of HBM per device.

v0:
```python
import functools
import math

import jax
import jax.numpy as jnp
from jax import lax
from jax.experimental import pallas as pl
from jax.experimental.pallas import tpu as pltpu
from jax.sharding import PartitionSpec as P

HEAD_DIM = 128
KV_HEADS = 8
MESH = pl.DeviceIdType.MESH
VMEM_BYTES = 62 * 1024 * 1024

rope_base = 500000.0
norm_epsilon = 1e-05
masked_score = -1e30
LOG2E = 1.4426950408889634


def partner_2(block, axis, stride):
    count = lax.axis_size(axis)
    route = []
    for low in range(count):
        high = low | 1 << stride
        if high != low and high < count:
            route += [(low, high), (high, low)]
    return lax.ppermute(block, axis, route)


def turn_pairs(matrix, positions, first_pair):
    pair_count = matrix.shape[-1] // 2
    pair_index = (first_pair + jnp.arange(pair_count, dtype=jnp.int32)).astype(jnp.float32)
    inverse_rates = rope_base ** (-2.0 * pair_index / HEAD_DIM)
    angles = positions.astype(jnp.float32)[:, None] * inverse_rates[None, :]
    cosine = jnp.cos(angles)[:, None, :]
    sine_part = jnp.sin(angles)[:, None, :]
    paired = matrix.reshape(matrix.shape[0], matrix.shape[1], pair_count, 2)
    former = paired[..., 0]
    latter = paired[..., 1]
    turned = jnp.stack(
        [former * cosine - latter * sine_part, former * sine_part + latter * cosine], axis=-1
    )
    return turned.reshape(matrix.shape)


def project_any(checkpoint, norm_gain, query_weight, key_weight, value_weight, positions):
    rows = checkpoint.shape[0]
    heads = query_weight.shape[1] // HEAD_DIM
    key_columns = key_weight.shape[1]
    gathered = lax.all_gather(checkpoint, "tp", axis=1, tiled=True)
    widened = gathered.astype(jnp.float32)
    mean_square = jnp.mean(widened * widened, axis=-1, keepdims=True)
    normed = (widened * lax.rsqrt(mean_square + norm_epsilon) * norm_gain).astype(jnp.bfloat16)
    query_features = jnp.dot(normed, query_weight, preferred_element_type=jnp.float32)
    key_features = jnp.dot(normed, key_weight, preferred_element_type=jnp.float32)
    value_features = jnp.dot(normed, value_weight, preferred_element_type=jnp.float32)
    turned = turn_pairs(query_features.reshape(rows, heads, HEAD_DIM), positions, 0)
    queries = (turned * (LOG2E / math.sqrt(HEAD_DIM))).astype(jnp.bfloat16)
    sharing = lax.axis_size("tp") // KV_HEADS
    part_of_head = lax.axis_index("tp") % sharing
    key_part = turn_pairs(
        key_features.reshape(rows, 1, key_columns), positions, part_of_head * (key_columns // 2)
    )
    key_part = key_part.astype(jnp.bfloat16).reshape(rows, key_columns)
    own_pair = jnp.stack([key_part, value_features.astype(jnp.bfloat16)])
    key_value = own_pair
    if sharing == 2:
        partner = partner_2(own_pair, "tp", 0)
        lower_first = jnp.concatenate([own_pair, partner], axis=-1)
        upper_first = jnp.concatenate([partner, own_pair], axis=-1)
        key_value = jnp.where(part_of_head == 0, lower_first, upper_first)
    return (
        queries.reshape(rows, heads * HEAD_DIM),
        jnp.concatenate([key_value[0], key_value[1]], axis=-1),
    )


def flipped(me, offset):
    result = me
    for bit in (1, 2, 4):
        if offset & bit:
            result = result + bit - 2 * bit * lax.rem(lax.div(me, bit), 2)
    return result


def greet(axis, others):
    barrier = pltpu.get_barrier_semaphore()
    for other in others:
        pl.semaphore_signal(barrier, inc=1, device_id={axis: other}, device_id_type=MESH)
    pl.semaphore_wait(barrier, len(others))


def sender(axis, send_sems, recv_sems):
    used = []

    def make(source, target, other):
        index = len(used)
        copy = pltpu.make_async_remote_copy(
            src_ref=source,
            dst_ref=target,
            send_sem=send_sems.at[index],
            recv_sem=recv_sems.at[index],
            device_id={axis: other},
            device_id_type=MESH,
        )
        used.append(copy)
        return copy

    return make, used


def project_kernel(
    x_hbm, gain_ref, wq_hbm, wk_hbm, wv_hbm, cos_ref, sin_ref,
    q_ref, kv_ref,
    held, weights, gains, acc, scaled, squares, x_sem, w_sems, send_sems, recv_sems,
):
    me = lax.axis_index("tp")
    rows, depth = x_hbm.shape
    half = depth // 2
    q_cols = wq_hbm.shape[1]
    k_cols = wk_hbm.shape[1]
    sib, nx, ny = flipped(me, 1), flipped(me, 2), flipped(me, 4)
    x_copies = [
        pltpu.make_async_copy(x_hbm.at[:, pl.ds(h * half, half)], held.at[0, h], x_sem.at[h])
        for h in range(2)
    ]
    for copy in x_copies:
        copy.start()
    w_copies = []
    for e in range(8):
        chunk = pl.ds(pl.multiple_of(flipped(me, e) * depth, depth), depth)
        parts = (
            (wq_hbm, 0, q_cols),
            (wk_hbm, q_cols, k_cols),
            (wv_hbm, q_cols + k_cols, k_cols),
        )
        w_copies.append(
            [
                pltpu.make_async_copy(
                    w.at[chunk, :], weights.at[e, :, pl.ds(at, size)], w_sems.at[e, i]
                )
                for i, (w, at, size) in enumerate(parts)
            ]
        )
    for copies in w_copies:
        for copy in copies:
            copy.start()
    greet("tp", (sib, nx, ny))
    for copy in x_copies:
        copy.wait()
    make, used = sender("tp", send_sems, recv_sems)

    def part(slot, h):
        return held.at[slot, h]

    dx = [make(part(0, h), part(2, h), nx) for h in range(2)]
    dy = [make(part(0, h), part(4, h), ny) for h in range(2)]
    d1 = make(held.at[0], held.at[1], sib)
    forward_y = make(part(2, 0), part(6, 0), ny)
    forward_x = make(part(4, 1), part(6, 1), nx)
    d3 = [make(part(2, h), part(3, h), sib) for h in range(2)]
    d5 = [make(part(4, h), part(5, h), sib) for h in range(2)]
    d7 = [make(part(6, h), part(7, h), sib) for h in range(2)]
    dx[0].start()
    dy[1].start()
    dx[1].start()
    dy[0].start()
    d1.start()

    squares[...] = jnp.zeros_like(squares)
    acc[...] = jnp.zeros_like(acc)
    for e in range(8):
        at = pl.ds(pl.multiple_of(flipped(me, e) * depth, depth), depth)
        gains[e] = gain_ref[:, at]

    def process(e, h):
        @pl.loop(0, rows // 64)
        def _(i):
            at = pl.ds(pl.multiple_of(i * 64, 64), 64)
            wide = held[e, h, at, :].astype(jnp.float32)
            squares[at, :] += jnp.sum(wide * wide, axis=1, keepdims=True)
            gain = gains[e, :, h * half : (h + 1) * half]
            scaled[at, :] = (wide * gain).astype(jnp.bfloat16)

        @pl.loop(0, (q_cols + 2 * k_cols) // 256)
        def _(t):
            at = pl.ds(pl.multiple_of(t * 256, 256), 256)
            acc[:, at] += jnp.dot(
                scaled[...],
                weights[e, h * half : (h + 1) * half, at],
                preferred_element_type=jnp.float32,
            )

    def weights_of(*slots):
        for e in slots:
            for copy in w_copies[e]:
                copy.wait()

    weights_of(0)
    process(0, 0)
    process(0, 1)
    weights_of(1)
    d1.wait_recv()
    process(1, 0)
    process(1, 1)
    dx[0].wait_recv()
    forward_y.start()
    d3[0].start()
    dy[1].wait_recv()
    forward_x.start()
    d5[1].start()
    weights_of(2, 3, 4, 5)
    process(2, 0)
    process(4, 1)
    d3[0].wait_recv()
    process(3, 0)
    d5[1].wait_recv()
    process(5, 1)
    dx[1].wait_recv()
    d3[1].start()
    dy[0].wait_recv()
    d5[0].start()
    process(2, 1)
    process(4, 0)
    d3[1].wait_recv()
    process(3, 1)
    d5[0].wait_recv()
    process(5, 0)
    weights_of(6, 7)
    forward_y.wait_recv()
    d7[0].start()
    forward_x.wait_recv()
    d7[1].start()
    process(6, 0)
    process(6, 1)
    d7[0].wait_recv()
    process(7, 0)
    d7[1].wait_recv()
    process(7, 1)

    score_scale = LOG2E / math.sqrt(HEAD_DIM)
    features = depth * 8

    @pl.loop(0, rows // 64)
    def _(i):
        at = pl.ds(pl.multiple_of(i * 64, 64), 64)
        rate = lax.rsqrt(squares[at, :] * (1.0 / features) + norm_epsilon)
        cosine = cos_ref[at, :]
        sine = sin_ref[at, :]
        even = lax.rem(lax.broadcasted_iota(jnp.int32, (64, HEAD_DIM), 1), 2) == 0

        def turned(block):
            later = pltpu.roll(block, HEAD_DIM - 1, 1)
            former = pltpu.roll(block, 1, 1)
            return block * cosine + jnp.where(even, later, former) * sine

        for h in range(q_cols // HEAD_DIM):
            cols = pl.ds(h * HEAD_DIM, HEAD_DIM)
            q_ref[at, cols] = turned(acc[at, cols] * (rate * score_scale)).astype(jnp.bfloat16)
        keys = acc[at, pl.ds(q_cols, k_cols)] * rate
        kv_ref[at, pl.ds(0, k_cols)] = turned(keys).astype(jnp.bfloat16)
        values = acc[at, pl.ds(q_cols + k_cols, k_cols)] * rate
        kv_ref[at, pl.ds(k_cols, k_cols)] = values.astype(jnp.bfloat16)

    for copy in used:
        copy.wait_send()


def attend_kernel(
    n_cp, order_ref, q_ref, kv_hbm, out_ref, norm_ref,
    ring, extended, bias, top, weighted, norms, kv_sem, send_sems, recv_sems,
):
    me = lax.axis_index("cp")
    rows = q_ref.shape[0]
    block = rows // 2
    heads = q_ref.shape[1] // HEAD_DIM
    right, left = lax.rem(me + 1, n_cp), lax.rem(me + n_cp - 1, n_cp)
    own_copy = pltpu.make_async_copy(kv_hbm, ring.at[0], kv_sem)
    own_copy.start()
    greet("cp", (right, left))
    own_copy.wait()

    def hop(step, h):
        at = pl.ds(h * block, block)
        return pltpu.make_async_remote_copy(
            src_ref=ring.at[step, at, :],
            dst_ref=ring.at[step + 1, at, :],
            send_sem=send_sems.at[step, h],
            recv_sem=recv_sems.at[step, h],
            device_id={"cp": right},
            device_id_type=MESH,
        )

    hop(0, 0).start()
    hop(0, 1).start()
    extended[:, HEAD_DIM:] = jnp.ones((rows, HEAD_DIM), jnp.bfloat16)
    top[...] = jnp.full(top.shape, masked_score, jnp.float32)
    weighted[...] = jnp.zeros_like(weighted)

    def visit(step, carried):
        for h in range(2):

            @pl.when(step > 0)
            def _():
                hop(step - 1, h).wait_recv()

            @pl.when(jnp.logical_and(step > 0, step < n_cp - 1))
            def _():
                hop(step, h).start()

        owner = lax.rem(me - step + n_cp, n_cp)
        extended[:, :HEAD_DIM] = ring[step, :, HEAD_DIM:]
        base = lax.broadcasted_iota(jnp.int32, (block, block), 0) - lax.broadcasted_iota(
            jnp.int32, (block, block), 1
        )
        for i in range(2):
            for j in range(2):
                ahead = (order_ref[2 * me + i] - order_ref[2 * owner + j]) * block
                bias[i * block : (i + 1) * block, j * block : (j + 1) * block] = jnp.where(
                    base + ahead >= 0, 0.0, masked_score
                )

        def one_head(h, inner):
            cols = pl.ds(pl.multiple_of(h * HEAD_DIM, HEAD_DIM), HEAD_DIM)
            keys = ring[step, :, :HEAD_DIM]
            for i in range(2):
                at = pl.ds(i * block, block)
                scores = lax.dot_general(
                    q_ref[at, cols], keys, (((1,), (1,)), ((), ())),
                    preferred_element_type=jnp.float32,
                )
                scores = scores + bias[at, :]
                old_top = top[h, at, :]
                new_top = jnp.maximum(old_top, jnp.max(scores, axis=1, keepdims=True))
                weights = jnp.exp2(scores - new_top).astype(jnp.bfloat16)
                shrink = jnp.exp2(old_top - new_top)
                top[h, at, :] = new_top
                weighted[h, at, :] = weighted[h, at, :] * shrink + jnp.dot(
                    weights, extended[...], preferred_element_type=jnp.float32
                )
            return inner

        lax.fori_loop(0, heads, one_head, 0, unroll=2)
        return carried

    lax.fori_loop(0, n_cp, visit, 0)
    lane = lax.broadcasted_iota(jnp.int32, (rows, HEAD_DIM), 1)
    norms[...] = jnp.zeros_like(norms)
    for h in range(heads):
        totals = weighted[h, :, HEAD_DIM:]
        out_ref[:, h * HEAD_DIM : (h + 1) * HEAD_DIM] = (
            weighted[h, :, :HEAD_DIM] / totals
        ).astype(jnp.bfloat16)
        norm = (top[h] + jnp.log2(totals)) * (1.0 / LOG2E)
        norms[...] = jnp.where(lane == h, norm, norms[...])
    norm_ref[...] = jnp.transpose(norms[...])[:heads, :]

    for step in range(n_cp - 1):
        for h in range(2):
            hop(step, h).wait_send()


def output_kernel(
    a_ref, w_hbm, out_ref,
    weights, terms, sums, from_sib, from_six, from_x, from_y, w_sems, send_sems, recv_sems,
):
    me = lax.axis_index("tp")
    rows, depth = a_ref.shape
    cols = out_ref.shape[1]
    half = cols // 2
    sib, nx, ny = flipped(me, 1), flipped(me, 2), flipped(me, 4)
    order = [
        (7, 0), (6, 0), (7, 1), (6, 1), (3, 0), (2, 0), (5, 1), (4, 1),
        (3, 1), (2, 1), (5, 0), (4, 0), (1, 0), (0, 0), (1, 1), (0, 1),
    ]
    w_copies = {}
    for e, h in order:
        at = pl.ds(pl.multiple_of(flipped(me, e) * cols + h * half, half), half)
        w_copies[e, h] = pltpu.make_async_copy(w_hbm.at[:, at], weights.at[e, h], w_sems.at[e, h])
        w_copies[e, h].start()
    greet("tp", (sib, nx, ny))
    make, used = sender("tp", send_sems, recv_sems)
    to_sib = {
        (e, h): make(terms.at[e, h], from_sib.at[e // 2, h], sib) for e in (1, 3, 5, 7) for h in (0, 1)
    }
    six_x = make(sums.at[3, 0], from_six.at[0], nx)
    six_y = make(sums.at[3, 1], from_six.at[1], ny)
    to_x = [make(sums.at[1, h], from_x.at[h], nx) for h in (0, 1)]
    to_y = [make(sums.at[2, h], from_y.at[h], ny) for h in (0, 1)]

    def term(e, h):
        w_copies[e, h].wait()

        @pl.loop(0, half // 256)
        def _(t):
            at = pl.ds(pl.multiple_of(t * 256, 256), 256)
            terms[e, h, :, at] = jnp.dot(
                a_ref[...], weights[e, h, :, at], preferred_element_type=jnp.float32
            ).astype(jnp.bfloat16)

        if e % 2:
            to_sib[e, h].start()

    def summed(e, h, others, target):
        to_sib[e + 1, h].wait_recv()

        @pl.loop(0, rows // 64)
        def _(i):
            at = pl.ds(pl.multiple_of(i * 64, 64), 64)
            total = terms[e, h, at, :].astype(jnp.float32)
            total = total + from_sib[e // 2, h, at, :].astype(jnp.float32)
            for other in others:
                total = total + other[at, :].astype(jnp.float32)
            target[at, :] = total.astype(jnp.bfloat16)

    term(7, 0)
    term(6, 0)
    summed(6, 0, (), sums.at[3, 0])
    six_x.start()
    term(7, 1)
    term(6, 1)
    summed(6, 1, (), sums.at[3, 1])
    six_y.start()
    term(3, 0)
    term(2, 0)
    summed(2, 0, (), sums.at[1, 0])
    to_x[0].start()
    term(5, 1)
    term(4, 1)
    summed(4, 1, (), sums.at[2, 1])
    to_y[1].start()
    term(3, 1)
    term(2, 1)
    term(5, 0)
    term(4, 0)
    six_x.wait_recv()
    summed(4, 0, (from_six.at[0],), sums.at[2, 0])
    to_y[0].start()
    six_y.wait_recv()
    summed(2, 1, (from_six.at[1],), sums.at[1, 1])
    to_x[1].start()
    term(1, 0)
    term(0, 0)
    term(1, 1)
    term(0, 1)
    for h in (0, 1):
        to_x[h].wait_recv()
        to_y[h].wait_recv()
        summed(0, h, (from_x.at[h], from_y.at[h]), out_ref.at[:, pl.ds(h * half, half)])
    for copy in used:
        copy.wait_send()


def shards(
    n_cp, n_tp, checkpoint, norm_gain, query_weight, key_weight, value_weight, output_weight, block_order
):
    rows, depth = checkpoint.shape
    q_cols = query_weight.shape[1]
    k_cols = key_weight.shape[1]
    heads = q_cols // HEAD_DIM
    block = rows // 2
    context_rank = lax.axis_index("cp")
    own_blocks = lax.dynamic_slice_in_dim(block_order, 2 * context_rank, 2)
    offsets = jnp.arange(block, dtype=jnp.int32)
    positions = (own_blocks[:, None] * block + offsets[None, :]).reshape(rows)
    lanes = jnp.arange(HEAD_DIM, dtype=jnp.int32)
    rates = rope_base ** (-2.0 * (lanes // 2).astype(jnp.float32) / HEAD_DIM)
    angles = positions.astype(jnp.float32)[:, None] * rates[None, :]
    cosine = jnp.cos(angles)
    sine = jnp.where(lanes % 2 == 0, -1.0, 1.0)[None, :] * jnp.sin(angles)

    any_spec = pl.BlockSpec(memory_space=pl.ANY)
    vmem = pl.BlockSpec(memory_space=pltpu.VMEM)
    smem = pl.BlockSpec(memory_space=pltpu.SMEM)
    bf16, f32 = jnp.bfloat16, jnp.float32
    dma = pltpu.SemaphoreType.DMA

    if n_tp == 8:
        queries, key_value = pl.pallas_call(
            project_kernel,
            out_shape=(
                jax.ShapeDtypeStruct((rows, q_cols), bf16),
                jax.ShapeDtypeStruct((rows, 2 * k_cols), bf16),
            ),
            in_specs=[any_spec, vmem, any_spec, any_spec, any_spec, vmem, vmem],
            out_specs=(vmem, vmem),
            scratch_shapes=[
                pltpu.VMEM((8, 2, rows, depth // 2), bf16),
                pltpu.VMEM((8, depth, q_cols + 2 * k_cols), bf16),
                pltpu.VMEM((8, 1, depth), f32),
                pltpu.VMEM((rows, q_cols + 2 * k_cols), f32),
                pltpu.VMEM((rows, depth // 2), bf16),
                pltpu.VMEM((rows, 1), f32),
                dma((2,)),
                dma((8, 3)),
                dma((13,)),
                dma((13,)),
            ],
            compiler_params=pltpu.CompilerParams(
                collective_id=0, has_side_effects=True, vmem_limit_bytes=VMEM_BYTES
            ),
            name="project",
        )(
            checkpoint, norm_gain.reshape(1, -1), query_weight, key_weight, value_weight, cosine, sine
        )
    else:
        queries, key_value = project_any(
            checkpoint, norm_gain, query_weight, key_weight, value_weight, positions
        )

    attended, normalizer = pl.pallas_call(
        functools.partial(attend_kernel, n_cp),
        out_shape=(
            jax.ShapeDtypeStruct((rows, q_cols), bf16),
            jax.ShapeDtypeStruct((heads, rows), f32),
        ),
        in_specs=[smem, vmem, any_spec],
        out_specs=(vmem, vmem),
        scratch_shapes=[
            pltpu.VMEM((n_cp, rows, 2 * HEAD_DIM), bf16),
            pltpu.VMEM((rows, 2 * HEAD_DIM), bf16),
            pltpu.VMEM((rows, rows), f32),
            pltpu.VMEM((heads, rows, 1), f32),
            pltpu.VMEM((heads, rows, 2 * HEAD_DIM), f32),
            pltpu.VMEM((rows, HEAD_DIM), f32),
            dma,
            dma((n_cp - 1, 2)),
            dma((n_cp - 1, 2)),
        ],
        compiler_params=pltpu.CompilerParams(
            collective_id=1, has_side_effects=True, vmem_limit_bytes=VMEM_BYTES
        ),
        name="attend",
    )(block_order, queries, key_value)

    if n_tp != 8:
        partial_terms = jnp.dot(attended, output_weight, preferred_element_type=jnp.float32)
        projected = lax.psum_scatter(
            partial_terms.astype(bf16), "tp", scatter_dimension=1, tiled=True
        )
        return (projected, normalizer)

    out_cols = output_weight.shape[1] // n_tp
    half = out_cols // 2
    projected = pl.pallas_call(
        output_kernel,
        out_shape=jax.ShapeDtypeStruct((rows, out_cols), bf16),
        in_specs=[vmem, any_spec],
        out_specs=vmem,
        scratch_shapes=[
            pltpu.VMEM((8, 2, q_cols, half), bf16),
            pltpu.VMEM((8, 2, rows, half), bf16),
            pltpu.VMEM((4, 2, rows, half), bf16),
            pltpu.VMEM((4, 2, rows, half), bf16),
            pltpu.VMEM((2, rows, half), bf16),
            pltpu.VMEM((2, rows, half), bf16),
            pltpu.VMEM((2, rows, half), bf16),
            dma((8, 2)),
            dma((14,)),
            dma((14,)),
        ],
        compiler_params=pltpu.CompilerParams(
            collective_id=2, has_side_effects=True, vmem_limit_bytes=VMEM_BYTES
        ),
        name="project_out",
    )(attended, output_weight)
    return (projected, normalizer)


def solution(mesh):
    return jax.shard_map(
        functools.partial(shards, mesh.shape["cp"], mesh.shape["tp"]),
        mesh=mesh,
        in_specs=(
            P("cp", "tp"),
            P(),
            P(None, "tp"),
            P(None, "tp"),
            P(None, "tp"),
            P("tp", None),
            P(),
        ),
        out_specs=(P("cp", "tp"), P("tp", "cp")),
        check_vma=False,
    )
```

profile of v0, /device:TPU:0, one launch (start us, length us, event | category | flops | bytes accessed | tf_op | source)
XLA Modules:
  0.0 141.1 jit_solution(5110973949482261553)
XLA Ops:
  0.6 0.7 dynamic-slice_multiply_fusion
  1.4 0.1 convert_bitcast_fusion
  1.5 1.8 %fusion = (f32[512,128]{1,0:T(8,128)}, f32[512,128]{1,0:T(8,128)}) fusion(f32[128]{0:T(128)S(1)} %get-tuple-element.12, f32[128]{0:T(128)S(1)} %get-tuple-element.13, f32[512]{0:T(512)S(1)} %bitcast.5), kind=kLoop, calls=%fused_computation.2 | loop fusion | flops 131072 | bytes 527360 | tf_op jit(solution)/shard_map/mul | solution.py:472
  3.3 58.9 %project.1 = (bf16[512,1024]{1,0:T(8,128)(2,1)}, bf16[512,256]{1,0:T(8,128)(2,1)}) custom-call(bf16[512,1024]{1,0:T(8,128)(2,1)} %x_hbm.1, f32[1,8192]{1,0:T(1,128)} %bitcast.4, bf16[8192,1024]{1,0:T(8,128)(2,1)} %wq_hbm.1, bf16[8192,128]{1,0:T(8,128)(2,1)} %wk_hbm.1, bf16[8192,128]{1,0:T(8,128)(2,1)} %wv_hbm.1, f32[512,128]{1,0:T(8,128)} %get-tuple-element.11.cos_ref, ...), custom_call_target="tpu_custom_call" | custom-call | tf_op jit(solution)/shard_map/project/pallas_call | solution.py:481
  62.2 30.6 %attend.1 = (bf16[512,1024]{1,0:T(8,128)(2,1)}, f32[8,512]{1,0:T(8,128)}) custom-call(s32[8]{0:T(128)} %order_ref.1, bf16[512,1024]{1,0:T(8,128)(2,1)} %get-tuple-element.6.q_ref, bf16[512,256]{1,0:T(8,128)(2,1)} %get-tuple-element.7.kv_hbm), custom_call_target="tpu_custom_call" | custom-call | tf_op jit(solution)/shard_map/attend/pallas_call | solution.py:513
  92.8 0.0 copy-start
  92.8 45.4 %project_out.1 = bf16[512,1024]{1,0:T(8,128)(2,1)} custom-call(bf16[512,1024]{1,0:T(8,128)(2,1)} %get-tuple-element.8.a_ref, bf16[1024,8192]{1,0:T(8,128)(2,1)} %w_hbm.1), custom_call_target="tpu_custom_call" | custom-call | tf_op jit(solution)/shard_map/project_out/pallas_call | solution.py:547
  138.2 2.3 %copy.12 = bf16[512,1024]{1,0:T(8,128)(2,1)} copy(bf16[512,1024]{1,0:T(8,128)(2,1)} %project_out.1) | data formatting | bytes 2097152
  140.5 0.0 copy-done
  140.5 0.6 copy.13
  (2 shorter events, 0.0 us)
Async XLA Ops:
  92.8 47.7 %copy-start = (f32[8,512]{1,0:T(8,128)S(1)}, f32[8,512]{1,0:T(8,128)}, u32[]{:S(2)}) copy-start(f32[8,512]{1,0:T(8,128)} %get-tuple-element.17) | copy-start | bytes 49156
where the time goes:
time: 141 us
  Pallas kernels  135 us (96%)
  local copies, waits for them, and re-layouts  2.88 us (2%)
  other arithmetic  2.62 us (2%)
    pallas_call x1, Pallas kernels, shards(): pl.pallas_call(project_kernel, out_shape=(jax.ShapeDtypeStruct((rows, q_c...  58.9 us
    pallas_call x1, Pallas kernels, shards(): pl.pallas_call(output_kernel, out_shape=jax.ShapeDtypeStruct((rows, out_c...  45.4 us
    pallas_call x1, Pallas kernels, shards(): pl.pallas_call(functools.partial(attend_kernel, n_cp), out_shape=(jax.Sha...  30.6 us
    unnamed x5, local copies, waits for them, and re-layouts  2.88 us

commit v1 on v0

v1 whole, which is shorter than its diff:
```python
import functools
import math

import jax
import jax.numpy as jnp
import numpy as np
from jax import lax
from jax.experimental import pallas as pl
from jax.experimental.pallas import tpu as pltpu
from jax.sharding import PartitionSpec as P

HEAD_DIM = 128
KV_HEADS = 8
MESH = pl.DeviceIdType.MESH
VMEM_BYTES = 62 * 1024 * 1024
FUSED_BYTES = 67_000_000

rope_base = 500000.0
norm_epsilon = 1e-05
masked_score = -1e30
LOG2E = 1.4426950408889634


def partner_2(block, axis, stride):
    count = lax.axis_size(axis)
    route = []
    for low in range(count):
        high = low | 1 << stride
        if high != low and high < count:
            route += [(low, high), (high, low)]
    return lax.ppermute(block, axis, route)


def turn_pairs(matrix, positions, first_pair):
    pair_count = matrix.shape[-1] // 2
    pair_index = (first_pair + jnp.arange(pair_count, dtype=jnp.int32)).astype(jnp.float32)
    inverse_rates = rope_base ** (-2.0 * pair_index / HEAD_DIM)
    angles = positions.astype(jnp.float32)[:, None] * inverse_rates[None, :]
    cosine = jnp.cos(angles)[:, None, :]
    sine_part = jnp.sin(angles)[:, None, :]
    paired = matrix.reshape(matrix.shape[0], matrix.shape[1], pair_count, 2)
    former = paired[..., 0]
    latter = paired[..., 1]
    turned = jnp.stack(
        [former * cosine - latter * sine_part, former * sine_part + latter * cosine], axis=-1
    )
    return turned.reshape(matrix.shape)


def project_any(checkpoint, norm_gain, query_weight, key_weight, value_weight, positions):
    rows = checkpoint.shape[0]
    heads = query_weight.shape[1] // HEAD_DIM
    key_columns = key_weight.shape[1]
    gathered = lax.all_gather(checkpoint, "tp", axis=1, tiled=True)
    widened = gathered.astype(jnp.float32)
    mean_square = jnp.mean(widened * widened, axis=-1, keepdims=True)
    normed = (widened * lax.rsqrt(mean_square + norm_epsilon) * norm_gain).astype(jnp.bfloat16)
    query_features = jnp.dot(normed, query_weight, preferred_element_type=jnp.float32)
    key_features = jnp.dot(normed, key_weight, preferred_element_type=jnp.float32)
    value_features = jnp.dot(normed, value_weight, preferred_element_type=jnp.float32)
    turned = turn_pairs(query_features.reshape(rows, heads, HEAD_DIM), positions, 0)
    queries = (turned * (LOG2E / math.sqrt(HEAD_DIM))).astype(jnp.bfloat16)
    sharing = lax.axis_size("tp") // KV_HEADS
    part_of_head = lax.axis_index("tp") % sharing
    key_part = turn_pairs(
        key_features.reshape(rows, 1, key_columns), positions, part_of_head * (key_columns // 2)
    )
    key_part = key_part.astype(jnp.bfloat16).reshape(rows, key_columns)
    own_pair = jnp.stack([key_part, value_features.astype(jnp.bfloat16)])
    key_value = own_pair
    if sharing == 2:
        partner = partner_2(own_pair, "tp", 0)
        lower_first = jnp.concatenate([own_pair, partner], axis=-1)
        upper_first = jnp.concatenate([partner, own_pair], axis=-1)
        key_value = jnp.where(part_of_head == 0, lower_first, upper_first)
    return (
        queries.reshape(rows, heads * HEAD_DIM),
        jnp.concatenate([key_value[0], key_value[1]], axis=-1),
    )


def flipped(me, offset):
    result = me
    for bit in (1, 2, 4):
        chosen = offset // bit % 2
        result = result + chosen * (bit - 2 * bit * (me // bit % 2))
    return result


def greet(axis, others):
    barrier = pltpu.get_barrier_semaphore()
    for other in others:
        pl.semaphore_signal(barrier, inc=1, device_id={axis: other}, device_id_type=MESH)
    pl.semaphore_wait(barrier, len(others))


def attend_kernel(
    n_cp, order_ref, q_ref, kv_hbm, out_ref, norm_ref,
    ring, extended, bias, top, weighted, norms, kv_sem, send_sems, recv_sems,
):
    me = lax.axis_index("cp")
    rows = q_ref.shape[0]
    block = rows // 2
    heads = q_ref.shape[1] // HEAD_DIM
    right, left = lax.rem(me + 1, n_cp), lax.rem(me + n_cp - 1, n_cp)
    own_copy = pltpu.make_async_copy(kv_hbm, ring.at[0], kv_sem)
    own_copy.start()
    greet("cp", (right, left))
    own_copy.wait()

    def hop(step, h):
        at = pl.ds(h * block, block)
        return pltpu.make_async_remote_copy(
            src_ref=ring.at[step, at, :],
            dst_ref=ring.at[step + 1, at, :],
            send_sem=send_sems.at[step, h],
            recv_sem=recv_sems.at[step, h],
            device_id={"cp": right},
            device_id_type=MESH,
        )

    hop(0, 0).start()
    hop(0, 1).start()
    extended[:, HEAD_DIM:] = jnp.ones((rows, HEAD_DIM), jnp.bfloat16)
    top[...] = jnp.full(top.shape, masked_score, jnp.float32)
    weighted[...] = jnp.zeros_like(weighted)

    def visit(step, carried):
        for h in range(2):

            @pl.when(step > 0)
            def _():
                hop(step - 1, h).wait_recv()

            @pl.when(jnp.logical_and(step > 0, step < n_cp - 1))
            def _():
                hop(step, h).start()

        owner = lax.rem(me - step + n_cp, n_cp)
        extended[:, :HEAD_DIM] = ring[step, :, HEAD_DIM:]
        base = lax.broadcasted_iota(jnp.int32, (block, block), 0) - lax.broadcasted_iota(
            jnp.int32, (block, block), 1
        )
        for i in range(2):
            for j in range(2):
                ahead = (order_ref[2 * me + i] - order_ref[2 * owner + j]) * block
                bias[i * block : (i + 1) * block, j * block : (j + 1) * block] = jnp.where(
                    base + ahead >= 0, 0.0, masked_score
                )

        def one_head(h, inner):
            cols = pl.ds(pl.multiple_of(h * HEAD_DIM, HEAD_DIM), HEAD_DIM)
            keys = ring[step, :, :HEAD_DIM]
            for i in range(2):
                at = pl.ds(i * block, block)
                scores = lax.dot_general(
                    q_ref[at, cols], keys, (((1,), (1,)), ((), ())),
                    preferred_element_type=jnp.float32,
                )
                scores = scores + bias[at, :]
                old_top = top[h, at, :]
                new_top = jnp.maximum(old_top, jnp.max(scores, axis=1, keepdims=True))
                weights = jnp.exp2(scores - new_top).astype(jnp.bfloat16)
                shrink = jnp.exp2(old_top - new_top)
                top[h, at, :] = new_top
                weighted[h, at, :] = weighted[h, at, :] * shrink + jnp.dot(
                    weights, extended[...], preferred_element_type=jnp.float32
                )
            return inner

        lax.fori_loop(0, heads, one_head, 0, unroll=2)
        return carried

    lax.fori_loop(0, n_cp, visit, 0)
    lane = lax.broadcasted_iota(jnp.int32, (rows, HEAD_DIM), 1)
    norms[...] = jnp.zeros_like(norms)
    for h in range(heads):
        totals = weighted[h, :, HEAD_DIM:]
        out_ref[:, h * HEAD_DIM : (h + 1) * HEAD_DIM] = (
            weighted[h, :, :HEAD_DIM] / totals
        ).astype(jnp.bfloat16)
        norm = (top[h] + jnp.log2(totals)) * (1.0 / LOG2E)
        norms[...] = jnp.where(lane == h, norm, norms[...])
    norm_ref[...] = jnp.transpose(norms[...])[:heads, :]

    for step in range(n_cp - 1):
        for h in range(2):
            hop(step, h).wait_send()


def layer_kernel(
    order_ref, x_hbm, gain_hbm, wq_hbm, wk_hbm, wv_hbm, wo_hbm, turns_hbm, starts_hbm,
    out_ref, norm_ref,
    held, weights, out_weights, gains, acc, scaled, squares, turns, starts,
    queries, keys, values, weighted, top, attended, from_sib, from_six, from_x, from_y,
    x_sems, w_sems, o_sems, t_sems, ag_send, ag_recv, kv_send, kv_recv, rs_send, rs_recv,
):
    me = lax.axis_index("tp")
    z = lax.axis_index("cp")
    rows, depth = x_hbm.shape
    half = depth // 2
    block = rows // 2
    q_cols = wq_hbm.shape[1]
    k_cols = wk_hbm.shape[1]
    heads = q_cols // HEAD_DIM
    kv_end = q_cols + 2 * k_cols
    sib, nx, ny = flipped(me, 1), flipped(me, 2), flipped(me, 4)
    pieces = ((0, block), (block, block // 2), (block + block // 2, block // 2))

    upper = z // 2
    low = z + upper * (3 - 2 * z)
    others = []
    for k in range(3):
        near = k + 1 - (low if k == 0 else 0)
        others.append(near + upper * (3 - 2 * near))

    def ring(k):
        near = k + 1 - low * ((3 - k) // 3)
        return near + upper * (3 - 2 * near)

    x_copies = []
    for p, (first, count) in enumerate(((0, block), (block, block))):
        for h in range(2):
            at = pl.ds(first, count)
            x_copies.append(
                pltpu.make_async_copy(
                    x_hbm.at[at, pl.ds(h * half, half)], held.at[0, h, at, :], x_sems.at[p, h]
                )
            )
    for copy in x_copies:
        copy.start()
    small = [
        pltpu.make_async_copy(gain_hbm, gains, t_sems.at[0]),
        pltpu.make_async_copy(turns_hbm, turns, t_sems.at[1]),
        pltpu.make_async_copy(starts_hbm, starts, t_sems.at[2]),
    ]
    small[0].start()
    w_copies = []
    for e in range(8):
        chunk = pl.ds(pl.multiple_of(flipped(me, e) * depth, depth), depth)
        parts = ((wq_hbm, 0, q_cols), (wk_hbm, q_cols, k_cols), (wv_hbm, q_cols + k_cols, k_cols))
        w_copies.append(
            [
                pltpu.make_async_copy(
                    w.at[chunk, :], weights.at[e, :, pl.ds(at, size)], w_sems.at[e, i]
                )
                for i, (w, at, size) in enumerate(parts)
            ]
        )
    for copies in w_copies:
        for copy in copies:
            copy.start()
    small[1].start()
    small[2].start()
    o_copies = {}
    for e in (7, 6, 3, 2, 5, 4, 1, 0):
        for h in range(2):
            at = pl.ds(pl.multiple_of(flipped(me, e) * depth + h * half, half), half)
            o_copies[e, h] = pltpu.make_async_copy(
                wo_hbm.at[:, at], out_weights.at[e, h], o_sems.at[e, h]
            )

    barrier = pltpu.get_barrier_semaphore()
    peers = [{"tp": sib}, {"tp": nx}, {"tp": ny}] + [{"cp": other} for other in others]
    for peer in peers:
        pl.semaphore_signal(barrier, inc=1, device_id=peer, device_id_type=MESH)
    pl.semaphore_wait(barrier, len(peers))

    def remote(source, target, send, recv, device):
        return pltpu.make_async_remote_copy(
            src_ref=source, dst_ref=target, send_sem=send, recv_sem=recv,
            device_id=device, device_id_type=MESH,
        )

    gather = []
    for p, (first, count) in enumerate(pieces):
        at = pl.ds(first, count)

        def part(slot, h, at=at):
            return held.at[slot, h, at, :]

        plan = {
            "dx0": (0, 0, 2, nx), "dx1": (0, 1, 2, nx), "dy0": (0, 0, 4, ny), "dy1": (0, 1, 4, ny),
            "s0": (0, 0, 1, sib), "s1": (0, 1, 1, sib), "fy": (2, 0, 6, ny), "fx": (4, 1, 6, nx),
            "a0": (2, 0, 3, sib), "a1": (2, 1, 3, sib), "b0": (4, 0, 5, sib), "b1": (4, 1, 5, sib),
            "c0": (6, 0, 7, sib), "c1": (6, 1, 7, sib),
        }
        gather.append(
            {
                name: remote(
                    part(slot, h), part(to, h), ag_send.at[p, i], ag_recv.at[p, i], {"tp": other}
                )
                for i, (name, (slot, h, to, other)) in enumerate(plan.items())
            }
        )

    def send(p, *names):
        for name in names:
            gather[p][name].start()

    def landed(p, *names):
        for name in names:
            gather[p][name].wait_recv()

    for copy in x_copies[:2]:
        copy.wait()
    send(0, "dx0", "dy1", "dx1", "dy0", "s0", "s1")
    acc[...] = jnp.zeros_like(acc)
    squares[...] = jnp.zeros_like(squares)
    values[:, HEAD_DIM:, :] = jnp.ones((4, 16, rows), jnp.bfloat16)
    for copy in x_copies[2:]:
        copy.wait()
    for p in (1, 2):
        send(p, "s0", "s1")
    small[0].wait()

    def weights_of(*slots):
        for e in slots:
            for copy in w_copies[e]:
                copy.wait()

    def process(first, count, chunks, chunk_of):
        @pl.loop(0, chunks)
        def _(i):
            e, h = chunk_of(i)
            source = flipped(me, e)

            @pl.loop(0, count // 64)
            def _(j):
                at = pl.ds(pl.multiple_of(first + j * 64, 64), 64)
                into = pl.ds(pl.multiple_of(j * 64, 64), 64)
                wide = held[e, h, at, :].astype(jnp.float32)
                squares[at, :] += jnp.sum(wide * wide, axis=1, keepdims=True)
                scaled[into, :] = (wide * gains[source, h]).astype(jnp.bfloat16)

            acc[first : first + count, :] += jnp.dot(
                scaled[:count, :],
                weights[e, pl.ds(pl.multiple_of(h * half, half), half), :],
                preferred_element_type=jnp.float32,
            )

    def own_pair(i):
        return i // 2, i % 2

    def early(i):
        return 2 + i, i // 2

    def late(i):
        return 2 + i, 1 - i // 2

    score_scale = LOG2E / math.sqrt(HEAD_DIM)
    features = depth * 8

    def exchange(p, k, which):
        first, count = pieces[p]
        if which == 0:
            ref = keys.at[z, pl.ds(first, count), :]
        else:
            ref = values.at[z, pl.ds(0, HEAD_DIM), pl.ds(first, count)]
        return remote(ref, ref, kv_send.at[p, k, which], kv_recv.at[p, z, which], {"cp": others[k]})

    def arrived(p, owner):
        first, count = pieces[p]
        refs = (
            keys.at[owner, pl.ds(first, count), :],
            values.at[owner, pl.ds(0, HEAD_DIM), pl.ds(first, count)],
        )
        for which, ref in enumerate(refs):
            remote(
                ref, ref, kv_send.at[p, 0, which], kv_recv.at[p, owner, which], {"cp": others[0]}
            ).wait_recv()

    def turner(first, j, sub):
        start = starts[order_ref[2 * z + first // block]]
        at = pl.ds(pl.multiple_of(first % block + j * sub, sub), sub)
        cosine = turns[0, at, :] * start[0:1, :] - turns[1, at, :] * start[1:2, :]
        sine = turns[1, at, :] * start[2:3, :] + turns[0, at, :] * start[3:4, :]
        even = lax.rem(lax.broadcasted_iota(jnp.int32, (sub, HEAD_DIM), 1), 2) == 0

        def turned(content):
            later = pltpu.roll(content, HEAD_DIM - 1, 1)
            former = pltpu.roll(content, 1, 1)
            return content * cosine + jnp.where(even, later, former) * sine

        return turned

    def rate_of(at):
        return lax.rsqrt(squares[at, :] * (1.0 / features) + norm_epsilon)

    def finish_keys(p):
        first, count = pieces[p]

        @pl.loop(0, count // 128)
        def _(j):
            at = pl.ds(pl.multiple_of(first + j * 128, 128), 128)
            rate = rate_of(at)
            turned = turner(first, j, 128)
            keys[z, at, :] = turned(acc[at, q_cols : q_cols + k_cols] * rate).astype(jnp.bfloat16)
            value = acc[at, q_cols + k_cols : kv_end] * rate
            values[z, :HEAD_DIM, at] = jnp.transpose(value).astype(jnp.bfloat16)

        for k in (2, 1, 0):
            for which in (0, 1):
                exchange(p, k, which).start()

    def finish_queries(p):
        first, count = pieces[p]

        @pl.loop(0, count // 64)
        def _(j):
            at = pl.ds(pl.multiple_of(first + j * 64, 64), 64)
            rate = rate_of(at) * score_scale
            turned = turner(first, j, 64)
            for h in range(heads):
                cols = pl.ds(h * HEAD_DIM, HEAD_DIM)
                queries[at, cols] = turned(acc[at, cols] * rate).astype(jnp.bfloat16)

    def visible(s, owner, j):
        ahead = order_ref[2 * z + s] - order_ref[2 * owner + j]
        return jnp.where(ahead > 0, 0.0, masked_score)

    def attend(s, owner, first, count, diagonal=False):
        q_at = pl.ds(s * block, block)
        shade = None if diagonal else visible(s, owner, first // block)

        def one_head(h, inner):
            cols = pl.ds(pl.multiple_of(h * HEAD_DIM, HEAD_DIM), HEAD_DIM)
            scores = lax.dot_general(
                keys[owner, pl.ds(first, count), :], queries[q_at, cols],
                (((1,), (1,)), ((), ())), preferred_element_type=jnp.float32,
            )
            slot = s * heads + h
            extended = values[owner, :, pl.ds(first, count)]
            if diagonal:
                key_at = lax.broadcasted_iota(jnp.int32, (count, block), 0)
                query_at = lax.broadcasted_iota(jnp.int32, (count, block), 1)
                scores = jnp.where(key_at <= query_at, scores, masked_score)
                new_top = jnp.max(scores, axis=0, keepdims=True)
                share = jnp.exp2(scores - new_top).astype(jnp.bfloat16)
                weighted[slot] = jnp.dot(extended, share, preferred_element_type=jnp.float32)
            else:
                old_top = top[slot]
                new_top = jnp.maximum(old_top, jnp.max(scores, axis=0, keepdims=True) + shade)
                share = jnp.exp2(scores - (new_top - shade)).astype(jnp.bfloat16)
                weighted[slot] = weighted[slot] * jnp.exp2(old_top - new_top) + jnp.dot(
                    extended, share, preferred_element_type=jnp.float32
                )
            top[slot] = new_top
            return inner

        lax.fori_loop(0, heads, one_head, 0, unroll=2)

    def attend_others(s, p, wait):
        first, count = pieces[p]

        @pl.loop(0, 3)
        def _(k):
            owner = ring(k)
            if wait:
                arrived(p, owner)
            attend(s, owner, first, count)

    def finish_heads(s):
        at = pl.ds(s * block, block)
        for h in range(heads):
            slot = s * heads + h
            totals = weighted[slot, HEAD_DIM : HEAD_DIM + 1, :]
            part = weighted[slot, :HEAD_DIM, :] * (1.0 / totals)
            attended[at, h * HEAD_DIM : (h + 1) * HEAD_DIM] = jnp.transpose(part).astype(
                jnp.bfloat16
            )
            norm_ref[h : h + 1, at] = (top[slot] + jnp.log2(totals)) * (1.0 / LOG2E)

    weights_of(0, 1)
    landed(0, "s0", "s1")
    process(*pieces[0], 4, own_pair)
    landed(0, "dx0")
    send(0, "fy", "a0")
    landed(0, "dy1")
    send(0, "fx", "b1")
    send(1, "dx0", "dy1", "dx1", "dy0")
    send(2, "dx0", "dy1")
    for copy in o_copies.values():
        copy.start()
    weights_of(2, 3, 4, 5)
    landed(0, "a0", "b1")
    process(*pieces[0], 4, early)
    landed(0, "dx1")
    send(0, "a1")
    landed(0, "dy0")
    send(0, "b0")
    for p in (1, 2):
        landed(p, "s0", "s1")
    process(block, block, 4, own_pair)
    landed(0, "a1", "b0")
    process(*pieces[0], 4, late)
    weights_of(6, 7)
    landed(0, "fy")
    send(0, "c0")
    landed(0, "fx")
    send(0, "c1")
    process(*pieces[0], 2, lambda i: (6, i))
    landed(0, "c0", "c1")
    process(*pieces[0], 2, lambda i: (7, i))
    small[1].wait()
    small[2].wait()
    finish_keys(0)
    landed(1, "dx0")
    send(1, "fy", "a0")
    landed(1, "dy1")
    send(1, "fx", "b1")
    send(2, "dx1", "dy0")
    finish_queries(0)
    attend(0, z, 0, block, diagonal=True)
    landed(1, "a0", "b1")
    process(*pieces[1], 4, early)
    landed(1, "dx1")
    send(1, "a1")
    landed(1, "dy0")
    send(1, "b0")
    landed(1, "a1", "b0")
    process(*pieces[1], 4, late)
    landed(2, "dx0")
    send(2, "fy", "a0")
    landed(2, "dy1")
    send(2, "fx", "b1")
    landed(2, "a0", "b1")
    process(*pieces[2], 4, early)
    landed(1, "fy")
    send(1, "c0")
    landed(1, "fx")
    send(1, "c1")
    process(*pieces[1], 2, lambda i: (6, i))
    landed(1, "c0", "c1")
    process(*pieces[1], 2, lambda i: (7, i))
    finish_keys(1)
    finish_queries(1)
    landed(2, "dx1")
    send(2, "a1")
    landed(2, "dy0")
    send(2, "b0")
    landed(2, "a1", "b0")
    process(*pieces[2], 4, late)
    landed(2, "fy")
    send(2, "c0")
    landed(2, "fx")
    send(2, "c1")
    process(*pieces[2], 2, lambda i: (6, i))
    landed(2, "c0", "c1")
    process(*pieces[2], 2, lambda i: (7, i))
    finish_keys(2)
    finish_queries(2)

    attend(0, z, block, block)
    attend(1, z, block, block, diagonal=True)
    attend(1, z, 0, block)
    attend_others(0, 0, True)
    attend_others(1, 0, False)
    attend_others(0, 1, True)
    attend_others(1, 1, False)
    for p in range(3):
        for copy in gather[p].values():
            copy.wait_send()
    attend_others(0, 2, True)
    finish_heads(0)

    scatter = []
    for s in range(2):
        at = pl.ds(s * block, block)
        plan = {}
        for e in (1, 3, 5, 7):
            for h in range(2):
                plan["s", e, h] = (held.at[e, h, at, :], from_sib.at[e // 2, h, at, :], sib)
        plan["six", 0] = (held.at[6, 0, at, :], from_six.at[0, at, :], nx)
        plan["six", 1] = (held.at[6, 1, at, :], from_six.at[1, at, :], ny)
        for h in range(2):
            plan["x", h] = (held.at[2, h, at, :], from_x.at[h, at, :], nx)
            plan["y", h] = (held.at[4, h, at, :], from_y.at[h, at, :], ny)
        scatter.append(
            {
                name: remote(source, target, rs_send.at[s, i], rs_recv.at[s, i], {"tp": other})
                for i, (name, (source, target, other)) in enumerate(plan.items())
            }
        )

    def term(s, e, h):
        if s == 0:
            o_copies[e, h].wait()
        at = pl.ds(s * block, block)
        held[e, h, at, :] = jnp.dot(
            attended[at, :], out_weights[e, h], preferred_element_type=jnp.float32
        ).astype(jnp.bfloat16)
        if e % 2:
            scatter[s]["s", e, h].start()

    def summed(s, e, h, more=()):
        scatter[s]["s", e + 1, h].wait_recv()

        @pl.loop(0, block // 64)
        def _(i):
            at = pl.ds(pl.multiple_of(s * block + i * 64, 64), 64)
            total = held[e, h, at, :].astype(jnp.float32)
            total = total + from_sib[e // 2, h, at, :].astype(jnp.float32)
            for other in more:
                total = total + other[at, :].astype(jnp.float32)
            if e:
                held[e, h, at, :] = total.astype(jnp.bfloat16)
            else:
                out_ref[at, h * half : (h + 1) * half] = total.astype(jnp.bfloat16)

    def far(s):
        term(s, 7, 0)
        term(s, 6, 0)
        term(s, 7, 1)
        summed(s, 6, 0)
        scatter[s]["six", 0].start()
        term(s, 6, 1)
        term(s, 3, 0)
        summed(s, 6, 1)
        scatter[s]["six", 1].start()
        term(s, 2, 0)
        term(s, 5, 1)
        summed(s, 2, 0)
        scatter[s]["x", 0].start()
        term(s, 4, 1)
        term(s, 3, 1)
        summed(s, 4, 1)
        scatter[s]["y", 1].start()

    def near(s):
        term(s, 2, 1)
        term(s, 5, 0)
        term(s, 4, 0)
        scatter[s]["six", 0].wait_recv()
        summed(s, 4, 0, (from_six.at[0],))
        scatter[s]["y", 0].start()
        scatter[s]["six", 1].wait_recv()
        summed(s, 2, 1, (from_six.at[1],))
        scatter[s]["x", 1].start()

    def last(s):
        for h in range(2):
            scatter[s]["x", h].wait_recv()
            scatter[s]["y", h].wait_recv()
            summed(s, 0, h, (from_x.at[h], from_y.at[h]))

    far(0)
    attend_others(1, 2, False)
    finish_heads(1)
    near(0)
    far(1)
    for s in range(2):
        for h in range(2):
            term(s, 1, h)
            term(s, 0, h)
    near(1)
    last(0)
    last(1)
    for p in range(3):
        for k in range(3):
            for which in range(2):
                exchange(p, k, which).wait_send()
    for s in range(2):
        for copy in scatter[s].values():
            copy.wait_send()


def rotary_tables(block, count):
    lanes = np.arange(HEAD_DIM)
    rates = rope_base ** (-2.0 * (lanes // 2) / HEAD_DIM)
    sign = np.where(lanes % 2 == 0, -1.0, 1.0)
    inside = np.arange(block)[:, None] * rates[None, :]
    turns = np.stack([np.cos(inside), np.sin(inside)]).astype(np.float32)
    begin = (np.arange(count) * block)[:, None] * rates[None, :]
    cosine, sine = np.cos(begin), np.sin(begin)
    starts = np.stack([cosine, sine, sign * cosine, sign * sine], axis=1)
    starts = np.concatenate([starts, np.zeros_like(starts)], axis=1).astype(np.float32)
    return jnp.asarray(turns), jnp.asarray(starts)


def fused_shards(
    n_cp, n_tp, checkpoint, norm_gain, query_weight, key_weight, value_weight, output_weight, block_order
):
    rows, depth = checkpoint.shape
    q_cols = query_weight.shape[1]
    k_cols = key_weight.shape[1]
    heads = q_cols // HEAD_DIM
    block = rows // 2
    half = depth // 2
    bf16, f32 = jnp.bfloat16, jnp.float32
    turns, starts = rotary_tables(block, block_order.shape[0])
    any_spec = pl.BlockSpec(memory_space=pl.ANY)
    vmem = pl.BlockSpec(memory_space=pltpu.VMEM)
    smem = pl.BlockSpec(memory_space=pltpu.SMEM)
    dma = pltpu.SemaphoreType.DMA
    return pl.pallas_call(
        layer_kernel,
        out_shape=(
            jax.ShapeDtypeStruct((rows, depth), bf16),
            jax.ShapeDtypeStruct((heads, rows), f32),
        ),
        in_specs=[smem] + [any_spec] * 8,
        out_specs=(vmem, vmem),
        scratch_shapes=[
            pltpu.VMEM((8, 2, rows, half), bf16),
            pltpu.VMEM((8, depth, q_cols + 2 * k_cols), bf16),
            pltpu.VMEM((8, 2, q_cols, half), bf16),
            pltpu.VMEM((8, 2, 1, half), f32),
            pltpu.VMEM((rows, q_cols + 2 * k_cols), f32),
            pltpu.VMEM((block, half), bf16),
            pltpu.VMEM((rows, 1), f32),
            pltpu.VMEM((2, block, HEAD_DIM), f32),
            pltpu.VMEM(starts.shape, f32),
            pltpu.VMEM((rows, q_cols), bf16),
            pltpu.VMEM((n_cp, rows, HEAD_DIM), bf16),
            pltpu.VMEM((n_cp, HEAD_DIM + 16, rows), bf16),
            pltpu.VMEM((2 * heads, HEAD_DIM + 16, block), f32),
            pltpu.VMEM((2 * heads, 1, block), f32),
            pltpu.VMEM((rows, q_cols), bf16),
            pltpu.VMEM((4, 2, rows, half), bf16),
            pltpu.VMEM((2, rows, half), bf16),
            pltpu.VMEM((2, rows, half), bf16),
            pltpu.VMEM((2, rows, half), bf16),
            dma((2, 2)),
            dma((8, 3)),
            dma((8, 2)),
            dma((3,)),
            dma((3, 14)),
            dma((3, 14)),
            dma((3, n_cp - 1, 2)),
            dma((3, n_cp, 2)),
            dma((2, 14)),
            dma((2, 14)),
        ],
        compiler_params=pltpu.CompilerParams(
            collective_id=0, has_side_effects=True, vmem_limit_bytes=FUSED_BYTES
        ),
        name="layer",
    )(
        block_order, checkpoint, norm_gain.reshape(8, 2, 1, half), query_weight, key_weight,
        value_weight, output_weight, turns, starts,
    )


def shards(
    n_cp, n_tp, checkpoint, norm_gain, query_weight, key_weight, value_weight, output_weight, block_order
):
    rows = checkpoint.shape[0]
    q_cols = query_weight.shape[1]
    heads = q_cols // HEAD_DIM
    block = rows // 2
    context_rank = lax.axis_index("cp")
    own_blocks = lax.dynamic_slice_in_dim(block_order, 2 * context_rank, 2)
    offsets = jnp.arange(block, dtype=jnp.int32)
    positions = (own_blocks[:, None] * block + offsets[None, :]).reshape(rows)

    vmem = pl.BlockSpec(memory_space=pltpu.VMEM)
    smem = pl.BlockSpec(memory_space=pltpu.SMEM)
    bf16, f32 = jnp.bfloat16, jnp.float32
    dma = pltpu.SemaphoreType.DMA
    queries, key_value = project_any(
        checkpoint, norm_gain, query_weight, key_weight, value_weight, positions
    )
    attended, normalizer = pl.pallas_call(
        functools.partial(attend_kernel, n_cp),
        out_shape=(
            jax.ShapeDtypeStruct((rows, q_cols), bf16),
            jax.ShapeDtypeStruct((heads, rows), f32),
        ),
        in_specs=[smem, vmem, pl.BlockSpec(memory_space=pl.ANY)],
        out_specs=(vmem, vmem),
        scratch_shapes=[
            pltpu.VMEM((n_cp, rows, 2 * HEAD_DIM), bf16),
            pltpu.VMEM((rows, 2 * HEAD_DIM), bf16),
            pltpu.VMEM((rows, rows), f32),
            pltpu.VMEM((heads, rows, 1), f32),
            pltpu.VMEM((heads, rows, 2 * HEAD_DIM), f32),
            pltpu.VMEM((rows, HEAD_DIM), f32),
            dma,
            dma((n_cp - 1, 2)),
            dma((n_cp - 1, 2)),
        ],
        compiler_params=pltpu.CompilerParams(
            collective_id=1, has_side_effects=True, vmem_limit_bytes=VMEM_BYTES
        ),
        name="attend",
    )(block_order, queries, key_value)
    partial_terms = jnp.dot(attended, output_weight, preferred_element_type=jnp.float32)
    projected = lax.psum_scatter(partial_terms.astype(bf16), "tp", scatter_dimension=1, tiled=True)
    return (projected, normalizer)


def solution(mesh):
    n_cp, n_tp = mesh.shape["cp"], mesh.shape["tp"]
    body = fused_shards if (n_cp, n_tp) == (4, 8) else shards
    return jax.shard_map(
        functools.partial(body, n_cp, n_tp),
        mesh=mesh,
        in_specs=(
            P("cp", "tp"),
            P(),
            P(None, "tp"),
            P(None, "tp"),
            P(None, "tp"),
            P("tp", None),
            P(),
        ),
        out_specs=(P("cp", "tp"), P("tp", "cp")),
        check_vma=False,
    )
```

time: 141 us -> 152 us (1.078)
  Pallas kernels: 135 us -> 148 us
  other arithmetic: 2.62 us -> 0 us
    pallas_call x3 -> x1, Pallas kernels: 135 us -> 148 us  [fused_shards(): pl.pallas_call(layer_kernel, out_shape=(jax.ShapeDtypeStruct((rows, depth...]
    mul x2 -> x0, other arithmetic: 2.54 us -> none  [the longest x1 1.8 us: shards(): sine = jnp.where(lanes % 2 == 0, -1.0, 1.0)[None, :] * jnp.sin(angles)]
    unnamed x5 -> x2, local copies, waits for them, and re-layouts: 2.88 us -> 3.59 us
where the time goes in v1:
time: 152 us
  Pallas kernels  148 us (97%)
  local copies, waits for them, and re-layouts  3.59 us (2%)
    pallas_call x1, Pallas kernels, fused_shards(): pl.pallas_call(layer_kernel, out_shape=(jax.ShapeDtypeStruct((rows, depth...  148 us
    unnamed x2, local copies, waits for them, and re-layouts  3.59 us

profile of v1, /device:TPU:0, one launch (start us, length us, event | category | flops | bytes accessed | tf_op | source)
XLA Modules:
  0.0 152.0 jit_solution(340330301781066177)
XLA Ops:
  0.6 147.8 %layer.1 = (bf16[512,1024]{1,0:T(8,128)(2,1)}, f32[8,512]{1,0:T(8,128)}) custom-call(s32[8]{0:T(128)} %order_ref.1, bf16[512,1024]{1,0:T(8,128)(2,1)} %x_hbm.1, f32[8,2,1,512]{3,2,1,0:T(1,128)} %bitcast.1, bf16[8192,1024]{1,0:T(8,128)(2,1)} %wq_hbm.1, bf16[8192,128]{1,0:T(8,128)(2,1)} %wk_hbm.1, bf16[8192,128]{1,0:T(8,128)(2,1)} %wv_hbm.1, ...), custom_call_target="tpu_custom_call" | custom-call | tf_op jit(solution)/shard_map/layer/pallas_call | solution.py:696
  148.4 2.3 %copy.13 = bf16[512,1024]{1,0:T(8,128)(2,1)} copy(bf16[512,1024]{1,0:T(8,128)(2,1)} %get-tuple-element.4) | data formatting | bytes 2097152
  150.7 1.3 copy.14

commit v2 on v1

--- a/solution.py
+++ b/solution.py
@@ -192,7 +192,7 @@
     order_ref, x_hbm, gain_hbm, wq_hbm, wk_hbm, wv_hbm, wo_hbm, turns_hbm, starts_hbm,
     out_ref, norm_ref,
     held, weights, out_weights, gains, acc, scaled, squares, turns, starts,
-    queries, keys, values, weighted, top, attended, from_sib, from_six, from_x, from_y,
+    queries, keys, values, weighted, top, from_sib, from_six, from_x, from_y,
     x_sems, w_sems, o_sems, t_sems, ag_send, ag_recv, kv_send, kv_recv, rs_send, rs_recv,
 ):
     me = lax.axis_index("tp")
@@ -213,10 +213,6 @@
     for k in range(3):
         near = k + 1 - (low if k == 0 else 0)
         others.append(near + upper * (3 - 2 * near))
-
-    def ring(k):
-        near = k + 1 - low * ((3 - k) // 3)
-        return near + upper * (3 - 2 * near)
 
     x_copies = []
     for p, (first, count) in enumerate(((0, block), (block, block))):
@@ -247,11 +243,6 @@
                 for i, (w, at, size) in enumerate(parts)
             ]
         )
-    for copies in w_copies:
-        for copy in copies:
-            copy.start()
-    small[1].start()
-    small[2].start()
     o_copies = {}
     for e in (7, 6, 3, 2, 5, 4, 1, 0):
         for h in range(2):
@@ -305,6 +296,11 @@
     for copy in x_copies[:2]:
         copy.wait()
     send(0, "dx0", "dy1", "dx1", "dy0", "s0", "s1")
+    for copies in w_copies:
+        for copy in copies:
+            copy.start()
+    small[1].start()
+    small[2].start()
     acc[...] = jnp.zeros_like(acc)
     squares[...] = jnp.zeros_like(squares)
     values[:, HEAD_DIM:, :] = jnp.ones((4, 16, rows), jnp.bfloat16)
@@ -419,57 +415,88 @@
         ahead = order_ref[2 * z + s] - order_ref[2 * owner + j]
         return jnp.where(ahead > 0, 0.0, masked_score)
 
-    def attend(s, owner, first, count, diagonal=False):
+    def attend(s, chunks, together, start=False, finish=False):
         q_at = pl.ds(s * block, block)
-        shade = None if diagonal else visible(s, owner, first // block)
-
-        def one_head(h, inner):
-            cols = pl.ds(pl.multiple_of(h * HEAD_DIM, HEAD_DIM), HEAD_DIM)
-            scores = lax.dot_general(
-                keys[owner, pl.ds(first, count), :], queries[q_at, cols],
-                (((1,), (1,)), ((), ())), preferred_element_type=jnp.float32,
-            )
+        shades = {}
+        for chunk in chunks:
+            for owner, first, count, diagonal in chunk:
+                if not diagonal:
+                    shades[id(owner), first] = visible(s, owner, first // block)
+
+        def columns(h):
+            return pl.ds(pl.multiple_of(h * HEAD_DIM, HEAD_DIM), HEAD_DIM)
+
+        def scored(h, side, j, peak):
+            offset = side * block
+            for owner, first, count, diagonal in chunks[j]:
+                scores = lax.dot_general(
+                    keys[owner, pl.ds(first, count), :], queries[q_at, columns(h)],
+                    (((1,), (1,)), ((), ())), preferred_element_type=jnp.float32,
+                )
+                if diagonal:
+                    key_at = lax.broadcasted_iota(jnp.int32, (count, block), 0)
+                    query_at = lax.broadcasted_iota(jnp.int32, (count, block), 1)
+                    scores = jnp.where(key_at <= query_at, scores, masked_score)
+                acc[offset : offset + count, j * block : (j + 1) * block] = scores
+                offset += count
+                highest = jnp.max(scores, axis=0, keepdims=True)
+                if not diagonal:
+                    highest = highest + shades[id(owner), first]
+                peak = highest if peak is None else jnp.maximum(peak, highest)
+            return peak
+
+        def beside(coming, side, h, peak):
             slot = s * heads + h
-            extended = values[owner, :, pl.ds(first, count)]
-            if diagonal:
-                key_at = lax.broadcasted_iota(jnp.int32, (count, block), 0)
-                query_at = lax.broadcasted_iota(jnp.int32, (count, block), 1)
-                scores = jnp.where(key_at <= query_at, scores, masked_score)
-                new_top = jnp.max(scores, axis=0, keepdims=True)
-                share = jnp.exp2(scores - new_top).astype(jnp.bfloat16)
-                weighted[slot] = jnp.dot(extended, share, preferred_element_type=jnp.float32)
+            new_top = peak
+            if not start:
+                old_top = top[slot]
+                new_top = jnp.maximum(old_top, peak)
+                shrink = jnp.exp2(old_top - new_top)
+            next_peak, total = None, None
+            for j, chunk in enumerate(chunks):
+                if coming is not None:
+                    next_peak = scored(coming, 1 - side, j, next_peak)
+                offset = side * block
+                shares, extended = [], []
+                for owner, first, count, diagonal in chunk:
+                    lean = new_top if diagonal else new_top - shades[id(owner), first]
+                    scores = acc[offset : offset + count, j * block : (j + 1) * block]
+                    shares.append(jnp.exp2(scores - lean).astype(jnp.bfloat16))
+                    extended.append(values[owner, :, pl.ds(first, count)])
+                    offset += count
+                share, wide = shares[0], extended[0]
+                if len(chunk) > 1:
+                    share, wide = jnp.concatenate(shares, 0), jnp.concatenate(extended, 1)
+                piece = jnp.dot(wide, share, preferred_element_type=jnp.float32)
+                total = piece if total is None else total + piece
+            if not start:
+                total = weighted[slot] * shrink + total
+            if finish:
+                sums = total[HEAD_DIM : HEAD_DIM + 1, :]
+                part = total[:HEAD_DIM, :] * (1.0 / sums)
+                queries[q_at, columns(h)] = jnp.transpose(part).astype(jnp.bfloat16)
+                norm_ref[pl.ds(h, 1), q_at] = (new_top + jnp.log2(sums)) * (1.0 / LOG2E)
             else:
-                old_top = top[slot]
-                new_top = jnp.maximum(old_top, jnp.max(scores, axis=0, keepdims=True) + shade)
-                share = jnp.exp2(scores - (new_top - shade)).astype(jnp.bfloat16)
-                weighted[slot] = weighted[slot] * jnp.exp2(old_top - new_top) + jnp.dot(
-                    extended, share, preferred_element_type=jnp.float32
-                )
-            top[slot] = new_top
-            return inner
-
-        lax.fori_loop(0, heads, one_head, 0, unroll=2)
-
-    def attend_others(s, p, wait):
-        first, count = pieces[p]
-
-        @pl.loop(0, 3)
-        def _(k):
-            owner = ring(k)
-            if wait:
-                arrived(p, owner)
-            attend(s, owner, first, count)
-
-    def finish_heads(s):
-        at = pl.ds(s * block, block)
-        for h in range(heads):
-            slot = s * heads + h
-            totals = weighted[slot, HEAD_DIM : HEAD_DIM + 1, :]
-            part = weighted[slot, :HEAD_DIM, :] * (1.0 / totals)
-            attended[at, h * HEAD_DIM : (h + 1) * HEAD_DIM] = jnp.transpose(part).astype(
-                jnp.bfloat16
-            )
-            norm_ref[h : h + 1, at] = (top[slot] + jnp.log2(totals)) * (1.0 / LOG2E)
+                weighted[slot] = total
+                top[slot] = new_top
+            return next_peak
+
+        peak = None
+        for j in range(len(chunks)):
+            peak = scored(0, 0, j, peak)
+        if together == heads:
+            for h in range(heads):
+                peak = beside(h + 1 if h + 1 < heads else None, h % 2, h, peak)
+        else:
+
+            def group(i, peak):
+                for u in range(together):
+                    h = i * together + u
+                    coming = h + 1 if u + 1 < together else jnp.minimum(h + 1, heads - 1)
+                    peak = beside(coming, u % 2, h, peak)
+                return peak
+
+            lax.fori_loop(0, heads // together, group, peak)
 
     weights_of(0, 1)
     landed(0, "s0", "s1")
@@ -511,7 +538,6 @@
     send(1, "fx", "b1")
     send(2, "dx1", "dy0")
     finish_queries(0)
-    attend(0, z, 0, block, diagonal=True)
     landed(1, "a0", "b1")
     process(*pieces[1], 4, early)
     landed(1, "dx1")
@@ -551,18 +577,38 @@
     finish_keys(2)
     finish_queries(2)
 
-    attend(0, z, block, block)
-    attend(1, z, block, block, diagonal=True)
-    attend(1, z, 0, block)
-    attend_others(0, 0, True)
-    attend_others(1, 0, False)
-    attend_others(0, 1, True)
-    attend_others(1, 1, False)
+    for owner in others:
+        arrived(0, owner)
+    third = block // 2
+    near, middle, distant = others
+    whole = [[(owner, 0, block, False)] for owner in others]
+    attend(0, [[(z, 0, block, True)]] + whole, 4, start=True)
+    attend(1, [[(z, block, block, True)], [(z, 0, block, False)]] + whole, 4, start=True)
+    for owner in others:
+        arrived(1, owner)
+    attend(
+        0,
+        [
+            [(z, block, block, False)],
+            [(near, block, third, False), (middle, block, third, False)],
+            [(distant, block, third, False)],
+        ],
+        4,
+    )
     for p in range(3):
         for copy in gather[p].values():
             copy.wait_send()
-    attend_others(0, 2, True)
-    finish_heads(0)
+    for owner in others:
+        arrived(2, owner)
+    attend(
+        0,
+        [
+            [(near, block + third, third, False), (middle, block + third, third, False)],
+            [(distant, block + third, third, False)],
+        ],
+        heads,
+        finish=True,
+    )
 
     scatter = []
     for s in range(2):
@@ -588,7 +634,7 @@
             o_copies[e, h].wait()
         at = pl.ds(s * block, block)
         held[e, h, at, :] = jnp.dot(
-            attended[at, :], out_weights[e, h], preferred_element_type=jnp.float32
+            queries[at, :], out_weights[e, h], preferred_element_type=jnp.float32
         ).astype(jnp.bfloat16)
         if e % 2:
             scatter[s]["s", e, h].start()
@@ -645,8 +691,7 @@
             summed(s, 0, h, (from_x.at[h], from_y.at[h]))
 
     far(0)
-    attend_others(1, 2, False)
-    finish_heads(1)
+    attend(1, [[(owner, block, block, False)] for owner in others], 4, finish=True)
     near(0)
     far(1)
     for s in range(2):
@@ -716,7 +761,6 @@
             pltpu.VMEM((n_cp, HEAD_DIM + 16, rows), bf16),
             pltpu.VMEM((2 * heads, HEAD_DIM + 16, block), f32),
             pltpu.VMEM((2 * heads, 1, block), f32),
-            pltpu.VMEM((rows, q_cols), bf16),
             pltpu.VMEM((4, 2, rows, half), bf16),
             pltpu.VMEM((2, rows, half), bf16),
             pltpu.VMEM((2, rows, half), bf16),

time: 152 us -> 108 us (0.71)
  Pallas kernels: 148 us -> 104 us
    pallas_call x1, Pallas kernels: 148 us -> 104 us  [fused_shards(): pl.pallas_call(layer_kernel, out_shape=(jax.ShapeDtypeStruct((rows, depth...]
where the time goes in v2:
time: 108 us
  Pallas kernels  104 us (96%)
  local copies, waits for them, and re-layouts  3.59 us (3%)
    pallas_call x1, Pallas kernels, fused_shards(): pl.pallas_call(layer_kernel, out_shape=(jax.ShapeDtypeStruct((rows, depth...  104 us
    unnamed x2, local copies, waits for them, and re-layouts  3.59 us

profile of v2, /device:TPU:0, one launch (start us, length us, event | category | flops | bytes accessed | tf_op | source)
XLA Modules:
  0.0 108.0 jit_solution(3092931761310131845)
XLA Ops:
  0.6 103.8 %layer.1 = (bf16[512,1024]{1,0:T(8,128)(2,1)}, f32[8,512]{1,0:T(8,128)}) custom-call(s32[8]{0:T(128)} %order_ref.1, bf16[512,1024]{1,0:T(8,128)(2,1)} %x_hbm.1, f32[8,2,1,512]{3,2,1,0:T(1,128)} %bitcast.1, bf16[8192,1024]{1,0:T(8,128)(2,1)} %wq_hbm.1, bf16[8192,128]{1,0:T(8,128)(2,1)} %wk_hbm.1, bf16[8192,128]{1,0:T(8,128)(2,1)} %wv_hbm.1, ...), custom_call_target="tpu_custom_call" | custom-call | tf_op jit(solution)/shard_map/layer/pallas_call | solution.py:741
  104.5 2.3 %copy.13 = bf16[512,1024]{1,0:T(8,128)(2,1)} copy(bf16[512,1024]{1,0:T(8,128)(2,1)} %get-tuple-element.4) | data formatting | bytes 2097152
  106.7 1.3 %copy.14 = f32[8,512]{1,0:T(8,128)} copy(f32[8,512]{1,0:T(8,128)} %get-tuple-element.5) | data formatting | bytes 32768

commit v3 on v2

--- a/solution.py
+++ b/solution.py
@@ -13,7 +13,7 @@
 KV_HEADS = 8
 MESH = pl.DeviceIdType.MESH
 VMEM_BYTES = 62 * 1024 * 1024
-FUSED_BYTES = 67_000_000
+FUSED_BYTES = 64_000_000
 
 rope_base = 500000.0
 norm_epsilon = 1e-05
@@ -189,9 +189,9 @@
 
 
 def layer_kernel(
-    order_ref, x_hbm, gain_hbm, wq_hbm, wk_hbm, wv_hbm, wo_hbm, turns_hbm, starts_hbm,
+    order_hbm, x_hbm, gain_hbm, wq_hbm, wk_hbm, wv_hbm, wo_hbm, turns_hbm, starts_hbm,
     out_ref, norm_ref,
-    held, weights, out_weights, gains, acc, scaled, squares, turns, starts,
+    order_ref, held, weights, out_weights, gains, acc, squares, turns, starts,
     queries, keys, values, weighted, top, from_sib, from_six, from_x, from_y,
     x_sems, w_sems, o_sems, t_sems, ag_send, ag_recv, kv_send, kv_recv, rs_send, rs_recv,
 ):
@@ -229,8 +229,10 @@
         pltpu.make_async_copy(gain_hbm, gains, t_sems.at[0]),
         pltpu.make_async_copy(turns_hbm, turns, t_sems.at[1]),
         pltpu.make_async_copy(starts_hbm, starts, t_sems.at[2]),
+        pltpu.make_async_copy(order_hbm, order_ref, t_sems.at[3]),
     ]
     small[0].start()
+    small[3].start()
     w_copies = []
     for e in range(8):
         chunk = pl.ds(pl.multiple_of(flipped(me, e) * depth, depth), depth)
@@ -315,23 +317,18 @@
             for copy in w_copies[e]:
                 copy.wait()
 
-    def process(first, count, chunks, chunk_of):
+    def process(first, count, chunks, chunk_of, low=0, high=kv_end):
+        at = pl.ds(first, count)
+
         @pl.loop(0, chunks)
         def _(i):
             e, h = chunk_of(i)
-            source = flipped(me, e)
-
-            @pl.loop(0, count // 64)
-            def _(j):
-                at = pl.ds(pl.multiple_of(first + j * 64, 64), 64)
-                into = pl.ds(pl.multiple_of(j * 64, 64), 64)
-                wide = held[e, h, at, :].astype(jnp.float32)
+            wide = held[e, h, at, :].astype(jnp.float32)
+            if high == kv_end:
                 squares[at, :] += jnp.sum(wide * wide, axis=1, keepdims=True)
-                scaled[into, :] = (wide * gains[source, h]).astype(jnp.bfloat16)
-
-            acc[first : first + count, :] += jnp.dot(
-                scaled[:count, :],
-                weights[e, pl.ds(pl.multiple_of(h * half, half), half), :],
+            acc[at, low:high] += jnp.dot(
+                (wide * gains[flipped(me, e), h]).astype(jnp.bfloat16),
+                weights[e, pl.ds(pl.multiple_of(h * half, half), half), low:high],
                 preferred_element_type=jnp.float32,
             )
 
@@ -426,8 +423,11 @@
         def columns(h):
             return pl.ds(pl.multiple_of(h * HEAD_DIM, HEAD_DIM), HEAD_DIM)
 
+        def place(side, j, offset, count):
+            return pl.ds(side * block + offset, count), pl.ds(j * block, block)
+
         def scored(h, side, j, peak):
-            offset = side * block
+            offset = 0
             for owner, first, count, diagonal in chunks[j]:
                 scores = lax.dot_general(
                     keys[owner, pl.ds(first, count), :], queries[q_at, columns(h)],
@@ -437,7 +437,7 @@
                     key_at = lax.broadcasted_iota(jnp.int32, (count, block), 0)
                     query_at = lax.broadcasted_iota(jnp.int32, (count, block), 1)
                     scores = jnp.where(key_at <= query_at, scores, masked_score)
-                acc[offset : offset + count, j * block : (j + 1) * block] = scores
+                acc[place(side, j, offset, count)] = scores
                 offset += count
                 highest = jnp.max(scores, axis=0, keepdims=True)
                 if not diagonal:
@@ -456,11 +456,11 @@
             for j, chunk in enumerate(chunks):
                 if coming is not None:
                     next_peak = scored(coming, 1 - side, j, next_peak)
-                offset = side * block
+                offset = 0
                 shares, extended = [], []
                 for owner, first, count, diagonal in chunk:
                     lean = new_top if diagonal else new_top - shades[id(owner), first]
-                    scores = acc[offset : offset + count, j * block : (j + 1) * block]
+                    scores = acc[place(side, j, offset, count)]
                     shares.append(jnp.exp2(scores - lean).astype(jnp.bfloat16))
                     extended.append(values[owner, :, pl.ds(first, count)])
                     offset += count
@@ -529,8 +529,8 @@
     process(*pieces[0], 2, lambda i: (6, i))
     landed(0, "c0", "c1")
     process(*pieces[0], 2, lambda i: (7, i))
-    small[1].wait()
-    small[2].wait()
+    for copy in small[1:]:
+        copy.wait()
     finish_keys(0)
     landed(1, "dx0")
     send(1, "fy", "a0")
@@ -561,6 +561,8 @@
     process(*pieces[1], 2, lambda i: (7, i))
     finish_keys(1)
     finish_queries(1)
+    third = block // 2
+    near, middle, distant = others
     landed(2, "dx1")
     send(2, "a1")
     landed(2, "dy0")
@@ -571,25 +573,22 @@
     send(2, "c0")
     landed(2, "fx")
     send(2, "c1")
-    process(*pieces[2], 2, lambda i: (6, i))
+    process(*pieces[2], 2, lambda i: (6, i), q_cols)
     landed(2, "c0", "c1")
-    process(*pieces[2], 2, lambda i: (7, i))
+    process(*pieces[2], 2, lambda i: (7, i), q_cols)
     finish_keys(2)
+    process(*pieces[2], 4, lambda i: (6 + i // 2, i % 2), 0, q_cols)
     finish_queries(2)
 
     for owner in others:
         arrived(0, owner)
-    third = block // 2
-    near, middle, distant = others
     whole = [[(owner, 0, block, False)] for owner in others]
-    attend(0, [[(z, 0, block, True)]] + whole, 4, start=True)
-    attend(1, [[(z, block, block, True)], [(z, 0, block, False)]] + whole, 4, start=True)
+    attend(0, [[(z, 0, block, True)], [(z, block, block, False)]] + whole, 4, start=True)
     for owner in others:
         arrived(1, owner)
     attend(
         0,
         [
-            [(z, block, block, False)],
             [(near, block, third, False), (middle, block, third, False)],
             [(distant, block, third, False)],
         ],
@@ -691,8 +690,9 @@
             summed(s, 0, h, (from_x.at[h], from_y.at[h]))
 
     far(0)
+    attend(1, [[(z, block, block, True)], [(z, 0, block, False)]] + whole, 4, start=True)
+    near(0)
     attend(1, [[(owner, block, block, False)] for owner in others], 4, finish=True)
-    near(0)
     far(1)
     for s in range(2):
         for h in range(2):
@@ -723,6 +723,17 @@
     return jnp.asarray(turns), jnp.asarray(starts)
 
 
+def store_kernel(out_ref, norm_ref, out_hbm, norm_hbm, sems):
+    copies = [
+        pltpu.make_async_copy(out_ref, out_hbm, sems.at[0]),
+        pltpu.make_async_copy(norm_ref, norm_hbm, sems.at[1]),
+    ]
+    for copy in copies:
+        copy.start()
+    for copy in copies:
+        copy.wait()
+
+
 def fused_shards(
     n_cp, n_tp, checkpoint, norm_gain, query_weight, key_weight, value_weight, output_weight, block_order
 ):
@@ -736,23 +747,19 @@
     turns, starts = rotary_tables(block, block_order.shape[0])
     any_spec = pl.BlockSpec(memory_space=pl.ANY)
     vmem = pl.BlockSpec(memory_space=pltpu.VMEM)
-    smem = pl.BlockSpec(memory_space=pltpu.SMEM)
     dma = pltpu.SemaphoreType.DMA
-    return pl.pallas_call(
+    results = pl.pallas_call(
         layer_kernel,
-        out_shape=(
-            jax.ShapeDtypeStruct((rows, depth), bf16),
-            jax.ShapeDtypeStruct((heads, rows), f32),
-        ),
-        in_specs=[smem] + [any_spec] * 8,
+        out_shape=(pltpu.VMEM((rows, depth), bf16), pltpu.VMEM((heads, rows), f32)),
+        in_specs=[any_spec] * 9,
         out_specs=(vmem, vmem),
         scratch_shapes=[
+            pltpu.SMEM(block_order.shape, jnp.int32),
             pltpu.VMEM((8, 2, rows, half), bf16),
             pltpu.VMEM((8, depth, q_cols + 2 * k_cols), bf16),
             pltpu.VMEM((8, 2, q_cols, half), bf16),
             pltpu.VMEM((8, 2, 1, half), f32),
             pltpu.VMEM((rows, q_cols + 2 * k_cols), f32),
-            pltpu.VMEM((block, half), bf16),
             pltpu.VMEM((rows, 1), f32),
             pltpu.VMEM((2, block, HEAD_DIM), f32),
             pltpu.VMEM(starts.shape, f32),
@@ -768,7 +775,7 @@
             dma((2, 2)),
             dma((8, 3)),
             dma((8, 2)),
-            dma((3,)),
+            dma((4,)),
             dma((3, 14)),
             dma((3, 14)),
             dma((3, n_cp - 1, 2)),
@@ -784,6 +791,18 @@
         block_order, checkpoint, norm_gain.reshape(8, 2, 1, half), query_weight, key_weight,
         value_weight, output_weight, turns, starts,
     )
+    return pl.pallas_call(
+        store_kernel,
+        out_shape=(
+            jax.ShapeDtypeStruct((rows, depth), bf16),
+            jax.ShapeDtypeStruct((heads, rows), f32),
+        ),
+        in_specs=[vmem, vmem],
+        out_specs=(any_spec, any_spec),
+        scratch_shapes=[dma((2,))],
+        compiler_params=pltpu.CompilerParams(vmem_limit_bytes=1 << 20),
+        name="store",
+    )(*results)
 
 
 def shards(

time: 108 us -> 96 us (0.89)
  Pallas kernels: 104 us -> 95 us
  local copies, waits for them, and re-layouts: 3.59 us -> 0 us
    pallas_call x1 -> x2, Pallas kernels: 104 us -> 95 us  [the longest x1 94 us: fused_shards(): pl.pallas_call(layer_kernel, out_shape=(pltpu.VMEM((rows, depth), bf16),...]
    unnamed x2 -> x0, local copies, waits for them, and re-layouts: 3.59 us -> none
where the time goes in v3:
time: 96 us; the launch traced here: 95.8 us
  Pallas kernels  95 us (99%)
    pallas_call x1, Pallas kernels, fused_shards(): pl.pallas_call(layer_kernel, out_shape=(pltpu.VMEM((rows, depth), bf16),...  94 us

profile of v3, /device:TPU:0, one launch (start us, length us, event | category | flops | bytes accessed | tf_op | source)
XLA Modules:
  0.0 95.8 jit_solution(8032520458232324561)
XLA Ops:
  0.6 94.0 %layer.1 = (bf16[512,1024]{1,0:T(8,128)(2,1)S(1)}, f32[8,512]{1,0:T(8,128)S(1)}) custom-call(s32[8]{0:T(128)} %order_hbm.1, bf16[512,1024]{1,0:T(8,128)(2,1)} %x_hbm.1, f32[8,2,1,512]{3,2,1,0:T(1,128)} %bitcast.1, bf16[8192,1024]{1,0:T(8,128)(2,1)} %wq_hbm.1, bf16[8192,128]{1,0:T(8,128)(2,1)} %wk_hbm.1, bf16[8192,128]{1,0:T(8,128)(2,1)} %wv_hbm.1, ...), custom_call_target="tpu_custom_call" | custom-call | tf_op jit(solution)/shard_map/layer/pallas_call | solution.py:751
  94.7 1.0 %store.1 = (bf16[512,1024]{1,0:T(8,128)(2,1)}, f32[8,512]{1,0:T(8,128)}) custom-call(bf16[512,1024]{1,0:T(8,128)(2,1)S(1)} %get-tuple-element.4.out_ref, f32[8,512]{1,0:T(8,128)S(1)} %get-tuple-element.5.norm_ref), custom_call_target="tpu_custom_call" | custom-call | tf_op jit(solution)/shard_map/store/pallas_call | solution.py:794

commit v4 on v3

--- a/solution.py
+++ b/solution.py
@@ -193,7 +193,7 @@
     out_ref, norm_ref,
     order_ref, held, weights, out_weights, gains, acc, squares, turns, starts,
     queries, keys, values, weighted, top, from_sib, from_six, from_x, from_y,
-    x_sems, w_sems, o_sems, t_sems, ag_send, ag_recv, kv_send, kv_recv, rs_send, rs_recv,
+    x_sems, w_sems, o_sems, t_sems, relay, ag_send, ag_recv, kv_send, kv_recv, rs_send, rs_recv,
 ):
     me = lax.axis_index("tp")
     z = lax.axis_index("cp")
@@ -254,10 +254,24 @@
             )
 
     barrier = pltpu.get_barrier_semaphore()
-    peers = [{"tp": sib}, {"tp": nx}, {"tp": ny}] + [{"cp": other} for other in others]
-    for peer in peers:
-        pl.semaphore_signal(barrier, inc=1, device_id=peer, device_id_type=MESH)
-    pl.semaphore_wait(barrier, len(peers))
+    inner = (z + 1) // 2 % 2
+
+    def tell(semaphore, device):
+        pl.semaphore_signal(semaphore, inc=1, device_id=device, device_id_type=MESH)
+
+    for other in (sib, nx, ny):
+        tell(barrier, {"tp": other})
+    tell(barrier, {"cp": others[0]})
+
+    @pl.when(inner == 1)
+    def _():
+        tell(barrier, {"cp": 3 - z})
+
+    pl.semaphore_wait(barrier, 4 + inner)
+
+    @pl.when(inner == 1)
+    def _():
+        tell(relay, {"cp": 3 - z})
 
     def remote(source, target, send, recv, device):
         return pltpu.make_async_remote_copy(
@@ -320,17 +334,21 @@
     def process(first, count, chunks, chunk_of, low=0, high=kv_end):
         at = pl.ds(first, count)
 
-        @pl.loop(0, chunks)
+        @pl.loop(0, chunks // 2)
         def _(i):
-            e, h = chunk_of(i)
-            wide = held[e, h, at, :].astype(jnp.float32)
-            if high == kv_end:
-                squares[at, :] += jnp.sum(wide * wide, axis=1, keepdims=True)
-            acc[at, low:high] += jnp.dot(
-                (wide * gains[flipped(me, e), h]).astype(jnp.bfloat16),
-                weights[e, pl.ds(pl.multiple_of(h * half, half), half), low:high],
-                preferred_element_type=jnp.float32,
-            )
+            total = None
+            for u in range(2):
+                e, h = chunk_of(2 * i + u)
+                wide = held[e, h, at, :].astype(jnp.float32)
+                if high == kv_end:
+                    squares[at, :] += jnp.sum(wide * wide, axis=1, keepdims=True)
+                piece = jnp.dot(
+                    (wide * gains[flipped(me, e), h]).astype(jnp.bfloat16),
+                    weights[e, pl.ds(pl.multiple_of(h * half, half), half), low:high],
+                    preferred_element_type=jnp.float32,
+                )
+                total = piece if total is None else total + piece
+            acc[at, low:high] += total
 
     def own_pair(i):
         return i // 2, i % 2
@@ -340,6 +358,9 @@
 
     def late(i):
         return 2 + i, 1 - i // 2
+
+    def last_two(i):
+        return 6 + i // 2, i % 2
 
     score_scale = LOG2E / math.sqrt(HEAD_DIM)
     features = depth * 8
@@ -392,7 +413,7 @@
             value = acc[at, q_cols + k_cols : kv_end] * rate
             values[z, :HEAD_DIM, at] = jnp.transpose(value).astype(jnp.bfloat16)
 
-        for k in (2, 1, 0):
+        for k in (0, 2, 1):
             for which in (0, 1):
                 exchange(p, k, which).start()
 
@@ -501,6 +522,12 @@
     weights_of(0, 1)
     landed(0, "s0", "s1")
     process(*pieces[0], 4, own_pair)
+
+    @pl.when(inner == 1)
+    def _():
+        pl.semaphore_wait(relay, 1)
+        tell(relay, {"cp": others[0]})
+
     landed(0, "dx0")
     send(0, "fy", "a0")
     landed(0, "dy1")
@@ -526,17 +553,23 @@
     send(0, "c0")
     landed(0, "fx")
     send(0, "c1")
-    process(*pieces[0], 2, lambda i: (6, i))
-    landed(0, "c0", "c1")
-    process(*pieces[0], 2, lambda i: (7, i))
+    process(*pieces[0], 2, lambda i: (6, i), q_cols)
     for copy in small[1:]:
         copy.wait()
+
+    @pl.when(inner == 0)
+    def _():
+        pl.semaphore_wait(relay, 1)
+
+    landed(0, "c0", "c1")
+    process(*pieces[0], 2, lambda i: (7, i), q_cols)
     finish_keys(0)
     landed(1, "dx0")
     send(1, "fy", "a0")
     landed(1, "dy1")
     send(1, "fx", "b1")
     send(2, "dx1", "dy0")
+    process(*pieces[0], 4, last_two, 0, q_cols)
     finish_queries(0)
     landed(1, "a0", "b1")
     process(*pieces[1], 4, early)
@@ -556,10 +589,11 @@
     send(1, "c0")
     landed(1, "fx")
     send(1, "c1")
-    process(*pieces[1], 2, lambda i: (6, i))
+    process(*pieces[1], 2, lambda i: (6, i), q_cols)
     landed(1, "c0", "c1")
-    process(*pieces[1], 2, lambda i: (7, i))
+    process(*pieces[1], 2, lambda i: (7, i), q_cols)
     finish_keys(1)
+    process(*pieces[1], 4, last_two, 0, q_cols)
     finish_queries(1)
     third = block // 2
     near, middle, distant = others
@@ -577,7 +611,7 @@
     landed(2, "c0", "c1")
     process(*pieces[2], 2, lambda i: (7, i), q_cols)
     finish_keys(2)
-    process(*pieces[2], 4, lambda i: (6 + i // 2, i % 2), 0, q_cols)
+    process(*pieces[2], 4, last_two, 0, q_cols)
     finish_queries(2)
 
     for owner in others:
@@ -655,22 +689,22 @@
 
     def far(s):
         term(s, 7, 0)
+        term(s, 7, 1)
         term(s, 6, 0)
-        term(s, 7, 1)
         summed(s, 6, 0)
         scatter[s]["six", 0].start()
         term(s, 6, 1)
-        term(s, 3, 0)
         summed(s, 6, 1)
         scatter[s]["six", 1].start()
+        term(s, 3, 0)
+        term(s, 5, 1)
         term(s, 2, 0)
-        term(s, 5, 1)
         summed(s, 2, 0)
         scatter[s]["x", 0].start()
         term(s, 4, 1)
-        term(s, 3, 1)
         summed(s, 4, 1)
         scatter[s]["y", 1].start()
+        term(s, 3, 1)
 
     def near(s):
         term(s, 2, 1)
@@ -776,6 +810,7 @@
             dma((8, 3)),
             dma((8, 2)),
             dma((4,)),
+            pltpu.SemaphoreType.REGULAR,
             dma((3, 14)),
             dma((3, 14)),
             dma((3, n_cp - 1, 2)),

time: 96 us -> 93.7 us (0.976)
  Pallas kernels: 95 us -> 92.7 us
    pallas_call x1, Pallas kernels: 94 us -> 91.7 us  [fused_shards(): pl.pallas_call(layer_kernel, out_shape=(pltpu.VMEM((rows, depth), bf16),...]
where the time goes in v4:
time: 93.7 us; the launch traced here: 93.5 us
  Pallas kernels  92.7 us (99%)
    pallas_call x1, Pallas kernels, fused_shards(): pl.pallas_call(layer_kernel, out_shape=(pltpu.VMEM((rows, depth), bf16),...  91.7 us

profile of v4, /device:TPU:0, one launch (start us, length us, event | category | flops | bytes accessed | tf_op | source)
XLA Modules:
  0.0 93.5 jit_solution(4633381776999555688)
XLA Ops:
  0.6 91.7 %layer.1 = (bf16[512,1024]{1,0:T(8,128)(2,1)S(1)}, f32[8,512]{1,0:T(8,128)S(1)}) custom-call(s32[8]{0:T(128)} %order_hbm.1, bf16[512,1024]{1,0:T(8,128)(2,1)} %x_hbm.1, f32[8,2,1,512]{3,2,1,0:T(1,128)} %bitcast.1, bf16[8192,1024]{1,0:T(8,128)(2,1)} %wq_hbm.1, bf16[8192,128]{1,0:T(8,128)(2,1)} %wk_hbm.1, bf16[8192,128]{1,0:T(8,128)(2,1)} %wv_hbm.1, ...), custom_call_target="tpu_custom_call" | custom-call | tf_op jit(solution)/shard_map/layer/pallas_call | solution.py:785
  92.4 1.0 %store.1 = (bf16[512,1024]{1,0:T(8,128)(2,1)}, f32[8,512]{1,0:T(8,128)}) custom-call(bf16[512,1024]{1,0:T(8,128)(2,1)S(1)} %get-tuple-element.4.out_ref, f32[8,512]{1,0:T(8,128)S(1)} %get-tuple-element.5.norm_ref), custom_call_target="tpu_custom_call" | custom-call | tf_op jit(solution)/shard_map/store/pallas_call | solution.py:829
